TPU v7x, 128 devices: a whole 4x4x4 slice. The times are simulated.
128 devices in a mesh: layer: 2 (over core), expert: 16 (over y, x), matrix: 4 (over z).
Axes of the slice: x: 4, y: 4, z: 4, core: 2. Of those that a mesh axis runs over, the one named last changes fastest.
Arguments:
- grads: float32 [32, 1, 2048, 768], P(('layer', 'expert'), None, 'matrix'), parts along dimension 0, may hold values from -6 to 6
- basis_out: float32 [32, 2048, 2048], P('layer', None, ('expert', 'matrix')), parts along dimension 0, may hold values from -0.125 to 0.125
- basis_in: float32 [32, 768, 768], P('layer', ('expert', 'matrix')), parts along dimension 0, may hold values from -0.21875 to 0.21875
- eigvals: float32 [32, 2048, 768], P('layer', ('expert', 'matrix')), parts along dimension 0, may hold values from 0.001 to 1
- counts: int32 [32], P(('layer', 'expert')), parts along dimension 0, may hold values from 0 to 1, as said below
- slot_query: int32 [32, 1], P(('layer', 'expert')), parts along dimension 0, may hold values from 0 to 31
Outputs:
- precond: float32 [32, 1, 2048, 768], P(('layer', 'expert'), None, 'matrix'), parts along dimension 0
- scores: float32 [64], P('layer'), parts along dimension 0
There are 2 independent parts, one for each index of `layer`. A program takes and returns all parts, laid end to end along the dimension named above; each array names one. Nothing has to cross between parts.
Inputs may be any that keep to these rules, and one draw needn't show every extreme that they name: `counts`: some expert has no live slot and some expert has all 1.
All inputs are finite; a program needn't handle non-finite values.
Results may differ from a plain program's by a relative error of at most 0.0003.
Values sent between devices are 32-bit elements; how exact they have to be, the bound alone decides.
A program may use at most 64 MiB of HBM per device.

v0:
```python
import jax
import jax.numpy as jnp
from jax import lax
from jax.sharding import PartitionSpec as P

QUERIES = 32
damping_fixed = 0.05
highest = lax.Precision.HIGHEST


def shards(grads, basis_out, basis_in, eigvals, counts, slot_query):
    capacity = grads.shape[1]
    own_rows = grads.shape[2]
    in_width = grads.shape[3]
    groups = lax.axis_size("matrix")
    columns = lax.all_to_all(basis_out, "expert", split_axis=0, concat_axis=2, tiled=True)[0]
    scales, inner = (
        lax.all_to_all(eigvals, "expert", split_axis=0, concat_axis=1, tiled=True),
        lax.all_to_all(basis_in, "expert", split_axis=0, concat_axis=1, tiled=True),
    )
    inner = lax.all_gather(inner, "matrix", axis=1, tiled=True)[0]
    sources = lax.axis_size("expert")
    inner = inner.reshape(groups, sources, -1, in_width).transpose(1, 0, 2, 3).reshape(-1, in_width)
    divisor = scales[0] + damping_fixed
    live_count = counts[0]
    queries = slot_query[0]
    local_rows = grads[0]
    slot_ids = jnp.arange(capacity, dtype=jnp.int32)
    live = (slot_ids < live_count).astype(jnp.float32)
    rotated = jnp.einsum(
        "ik,if->kf",
        columns,
        lax.all_gather(local_rows[0], "matrix", axis=0, tiled=True),
        precision=highest,
    )
    rotated = jnp.dot(rotated, inner, precision=highest)
    scaled = rotated / divisor
    back = jnp.einsum("kg,hg->kh", scaled, inner, precision=highest)

    def project_one(start, amount, back=back):
        return jnp.dot(columns, back, precision=highest)

    result = lax.psum_scatter(
        project_one(jnp.int32(0), own_rows * lax.axis_size("matrix")),
        "matrix",
        scatter_dimension=0,
        tiled=True,
    )
    results = [result * live[0]]
    precond = jnp.stack(results)
    values = jnp.sum(local_rows * precond, axis=(1, 2)) / (own_rows * groups * in_width)
    targets = jnp.arange(QUERIES, dtype=jnp.int32)
    onehot = (queries[:, None] == targets[None, :]).astype(jnp.float32)
    partial_scores = jnp.sum(values[:, None] * onehot, axis=0)
    scores = lax.psum(partial_scores, ("expert", "matrix"))
    return (precond[None], scores)


def solution(mesh):
    in_specs = (
        P(("layer", "expert"), None, "matrix", None),
        P("layer", None, ("expert", "matrix")),
        P("layer", ("expert", "matrix"), None),
        P("layer", ("expert", "matrix"), None),
        P(("layer", "expert")),
        P(("layer", "expert"), None),
    )
    out_specs = (P(("layer", "expert"), None, "matrix", None), P("layer"))
    return jax.shard_map(shards, mesh=mesh, in_specs=in_specs, out_specs=out_specs, check_vma=False)
```

profile of v0, /device:TPU:0, one launch (start us, length us, event | category | flops | bytes accessed | tf_op | source)
XLA Modules:
  0.0 419.3 jit_solution(11684869709950085901)
XLA Ops:
  7.2 1.4 copy.14
  8.6 21.3 %all_to_all.36 = f32[16,12,768]{2,1,0:T(8,128)S(1)} all-to-all(f32[16,12,768]{2,1,0:T(8,128)S(1)} %copy.14), channel_id=1, replica_groups=mesh['layer'=2,'expert'=16,'matrix'=4] {'expert'}, dimensions={0} | all-to-all | bytes 1179648 | tf_op jit(solution)/shard_map/all_to_all | solution.py:19
  29.9 0.9 all_to_all.31
  30.9 0.0 all-gather.6.cloned.1.call-start
  30.9 0.7 all-gather.6.cloned.1.call-update
  31.6 25.2 %all_to_all.37 = f32[16,32,768]{2,1,0:T(8,128)S(1)} all-to-all(f32[16,32,768]{2,1,0:T(8,128)S(1)} %copy-done.2), channel_id=1, replica_groups=mesh['layer'=2,'expert'=16,'matrix'=4] {'expert'}, dimensions={0} | all-to-all | bytes 3145728 | tf_op jit(solution)/shard_map/all_to_all | solution.py:18
  56.8 4.5 %all-to-all-start = ((f32[16,2048,32]{1,2,0:T(8,128)}), f32[16,2048,32]{1,2,0:T(8,128)}, u32[]{:S(2)}, u32[]{:S(2)}) async-start(f32[16,2048,32]{1,2,0:T(8,128)} %param.7), calls=%async_computation | async-start | bytes 8388608 | tf_op jit(solution)/shard_map/all_to_all | solution.py:16
  61.3 0.0 reduce-scatter.2.cloned.1.call-start
  61.4 1.3 broadcast_add_fusion
  62.7 2.4 reshape_squeeze.3
  65.1 2.0 copy.15
  67.2 2.6 reshape.33
  69.8 51.2 %all-to-all-done = f32[16,2048,32]{1,2,0:T(8,128)} async-done(((f32[16,2048,32]{1,2,0:T(8,128)}), f32[16,2048,32]{1,2,0:T(8,128)}, u32[]{:S(2)}, u32[]{:S(2)}) %all-to-all-start) | async-done | bytes 4194336 | tf_op jit(solution)/shard_map/all_to_all | solution.py:16
  121.0 9.2 %all-gather.6.cloned.1.call-done = f32[1,1,2048,768]{3,2,1,0:T(8,128)} async-done(((f32[1,1,512,768]{3,2,1,0:T(8,128)}), f32[1,1,2048,768]{3,2,1,0:T(8,128)}) %all-gather.6.cloned.1.call-update) | async-done | bytes 6291472 | tf_op jit(solution)/shard_map/all_gather | solution.py:33
  130.1 13.4 %fusion = f32[512,768]{1,0:T(8,128)S(1)} fusion(f32[2048,512]{0,1:T(8,128)} %bitcast.2, f32[1,1,2048,768]{3,2,1,0:T(8,128)} %all-gather.6.cloned.1.call-done), kind=kOutput, calls=%fused_computation | convolution fusion | flops 9663676416 | bytes 12058624 | tf_op jit(solution)/shard_map/ik,if->kf/dot_general | solution.py:30
  143.5 4.1 bitcast_divide_fusion
  147.6 4.0 fusion.3
  151.6 14.2 %convolution_bitcast_fusion = f32[2048,768]{0,1:T(8,128)} fusion(f32[512,768]{1,0:T(8,128)S(1)} %fusion.3, f32[2048,512]{0,1:T(8,128)} %bitcast.2), kind=kOutput, calls=%fused_computation.2 | convolution fusion | flops 9663676416 | bytes 12058624 | tf_op jit(solution)/shard_map/dot_general | solution.py:41
  165.8 1.4 copy-done
  167.2 0.5 copy.16
  168.9 61.7 %reduce-scatter.2.cloned.1.call-done = f32[512,768]{0,1:T(8,128)} async-done(((f32[2048,768]{0,1:T(8,128)}), f32[512,768]{0,1:T(8,128)}) %reduce-scatter.2.cloned.1.call-update) | async-done | bytes 1572880 | tf_op jit(solution)/shard_map/reduce_scatter | solution.py:43
  230.6 2.5 fusion.2
  233.1 1.6 copy.17
  235.5 177.3 %psum.7 = f32[32]{0:T(128)} all-reduce(f32[32]{0:T(128)S(1)} %compare_select_fusion), channel_id=1, replica_groups=mesh['layer'=2,'expert'=16,'matrix'=4] {'expert','matrix'}, use_global_device_ids=true, to_apply=%region_2.0 | all-reduce | flops 32 | bytes 256 | tf_op jit(solution)/shard_map/psum | solution.py:55
  (10 shorter events, 0.1 us)
Async XLA Ops:
  7.2 55.5 %all-gather.4.cloned.1.call-start = ((), (), s32[]{:S(2)}) async-start(), calls=%async_computation.4 | async-start | bytes 2949120 | tf_op jit(solution)/shard_map/all_gather | solution.py:21
  29.9 1.7 copy-start.2
  30.9 99.2 %all-gather.6.cloned.1.call-start = ((), (), s32[]{:S(2)}) async-start(), calls=%async_computation.6 | async-start | bytes 7864320 | tf_op jit(solution)/shard_map/all_gather | solution.py:33
  56.8 64.2 %all-to-all-start = ((f32[16,2048,32]{1,2,0:T(8,128)}), f32[16,2048,32]{1,2,0:T(8,128)}, u32[]{:S(2)}, u32[]{:S(2)}) async-start(f32[16,2048,32]{1,2,0:T(8,128)} %param.7), calls=%async_computation | async-start | bytes 8388608 | tf_op jit(solution)/shard_map/all_to_all | solution.py:16
  61.3 169.3 %reduce-scatter.2.cloned.1.call-start = ((), (), s32[]{:S(2)}) async-start(), calls=%async_computation.5 | async-start | bytes 7864320 | tf_op jit(solution)/shard_map/reduce_scatter | solution.py:43
  130.1 13.4 %copy-start.1 = (f32[16,32,768]{2,1,0:T(8,128)S(1)}, f32[16,32,768]{2,1,0:T(8,128)}, u32[]{:S(2)}) copy-start(f32[16,32,768]{2,1,0:T(8,128)} %broadcast_add_fusion) | copy-start | bytes 4718596
  165.8 1.4 copy-start
Sparse Core Ops, SparseCore 0:
  31.0 31.6 all-gather.3
  64.3 65.7 all-gather.5
  165.9 64.6 reduce-scatter.1
where the time goes:
time: 420 us; the launch traced here: 419 us
  blocking collectives  224 us (53%)
  waiting for transfers between devices  123 us (29%)
  matrix products  35.6 us (8%)
  between operations  15.8 us (4%)
  local copies, waits for them, and re-layouts  12.9 us (3%)
  starting transfers between devices  4.66 us (1%)
    psum x1, blocking collectives, shards(): scores = lax.psum(partial_scores, ('expert', 'matrix'))  177 us
    reduce_scatter x1, waiting for transfers between devices, shards(): lax.psum_scatter(project_one(jnp.int32(0), own_rows * lax.axis_size('matr...  61.7 us
    all_to_all x1, waiting for transfers between devices, shards(): lax.all_to_all(basis_out, 'expert', split_axis=0, concat_axis=2, tiled=True)  51.2 us
    all_to_all x1, blocking collectives, shards(): lax.all_to_all(eigvals, 'expert', split_axis=0, concat_axis=1, tiled=True)  25.2 us
    all_to_all x1, blocking collectives, shards(): lax.all_to_all(basis_in, 'expert', split_axis=0, concat_axis=1, tiled=True)  21.3 us
    dot_general x1, matrix products, project_one(): return jnp.dot(columns, back, precision=highest)  14.2 us
    dot_general x1, matrix products, shards(): jnp.einsum('ik,if->kf', columns, lax.all_gather(local_rows[0], 'matrix',...  13.4 us
    all_gather x1, waiting for transfers between devices, shards(): lax.all_gather(local_rows[0], 'matrix', axis=0, tiled=True)  9.16 us
  transfers between devices with their start and end apart: 4, of which 3 were waited for; matrix products, arithmetic and copies ran while one was open for 2% of the time, Pallas kernels for 0%

commit v1 on v0

--- a/solution.py
+++ b/solution.py
@@ -52,7 +52,7 @@
     targets = jnp.arange(QUERIES, dtype=jnp.int32)
     onehot = (queries[:, None] == targets[None, :]).astype(jnp.float32)
     partial_scores = jnp.sum(values[:, None] * onehot, axis=0)
-    scores = lax.psum(partial_scores, ("expert", "matrix"))
+    scores = lax.psum(lax.psum(partial_scores, axis_name="matrix"), "expert")
     return (precond[None], scores)
 
 

time: 420 us -> 292 us (0.70)
  blocking collectives: 224 us -> 95.7 us
    psum x1 -> x2, blocking collectives: 177 us -> 49.3 us  [shards(): scores = lax.psum(lax.psum(partial_scores, axis_name='matrix'), 'expert')]
  transfers between devices with their start and end apart: 4 -> 4, of which waited for: 3 -> 3; matrix products, arithmetic and copies ran while one was open for 2% -> 3% of each run, Pallas kernels for 0% -> 0%
where the time goes in v1:
time: 292 us; the launch traced here: 291 us
  waiting for transfers between devices  123 us (42%)
  blocking collectives  95.7 us (33%)
  matrix products  35.5 us (12%)
  between operations  15.7 us (5%)
  local copies, waits for them, and re-layouts  12.9 us (4%)
  starting transfers between devices  4.67 us (2%)
  other arithmetic  3.77 us (1%)
    reduce_scatter x1, waiting for transfers between devices, shards(): lax.psum_scatter(project_one(jnp.int32(0), own_rows * lax.axis_size('matr...  61.7 us
    all_to_all x1, waiting for transfers between devices, shards(): lax.all_to_all(basis_out, 'expert', split_axis=0, concat_axis=2, tiled=True)  51.2 us
    psum x2, blocking collectives, shards(): scores = lax.psum(lax.psum(partial_scores, axis_name='matrix'), 'expert')  49.3 us
    all_to_all x1, blocking collectives, shards(): lax.all_to_all(eigvals, 'expert', split_axis=0, concat_axis=1, tiled=True)  25.2 us
    all_to_all x1, blocking collectives, shards(): lax.all_to_all(basis_in, 'expert', split_axis=0, concat_axis=1, tiled=True)  21.3 us
    dot_general x1, matrix products, project_one(): return jnp.dot(columns, back, precision=highest)  14.1 us
    dot_general x1, matrix products, shards(): jnp.einsum('ik,if->kf', columns, lax.all_gather(local_rows[0], 'matrix',...  13.4 us
    all_gather x1, waiting for transfers between devices, shards(): lax.all_gather(local_rows[0], 'matrix', axis=0, tiled=True)  9.14 us
  transfers between devices with their start and end apart: 4, of which 3 were waited for; matrix products, arithmetic and copies ran while one was open for 3% of the time, Pallas kernels for 0%

profile of v1, /device:TPU:0, one launch (start us, length us, event | category | flops | bytes accessed | tf_op | source)
XLA Modules:
  0.0 291.1 jit_solution(16280962832654655030)
XLA Ops:
  7.2 1.4 copy.14
  8.6 21.3 %all_to_all.36 = f32[16,12,768]{2,1,0:T(8,128)S(1)} all-to-all(f32[16,12,768]{2,1,0:T(8,128)S(1)} %copy.14), channel_id=1, replica_groups=mesh['layer'=2,'expert'=16,'matrix'=4] {'expert'}, dimensions={0} | all-to-all | bytes 1179648 | tf_op jit(solution)/shard_map/all_to_all | solution.py:19
  29.9 0.9 all_to_all.31
  30.9 0.7 all-gather.6.cloned.1.call-update
  31.7 25.2 %all_to_all.37 = f32[16,32,768]{2,1,0:T(8,128)S(1)} all-to-all(f32[16,32,768]{2,1,0:T(8,128)S(1)} %copy-done.2), channel_id=1, replica_groups=mesh['layer'=2,'expert'=16,'matrix'=4] {'expert'}, dimensions={0} | all-to-all | bytes 3145728 | tf_op jit(solution)/shard_map/all_to_all | solution.py:18
  56.8 4.6 %all-to-all-start = ((f32[16,2048,32]{1,2,0:T(8,128)}), f32[16,2048,32]{1,2,0:T(8,128)}, u32[]{:S(2)}, u32[]{:S(2)}) async-start(f32[16,2048,32]{1,2,0:T(8,128)} %param.7), calls=%async_computation | async-start | bytes 8388608 | tf_op jit(solution)/shard_map/all_to_all | solution.py:16
  61.4 0.0 reduce-scatter.2.cloned.1.call-start
  61.4 1.3 broadcast_add_fusion
  62.7 2.4 reshape_squeeze.3
  65.2 2.0 copy.15
  67.2 2.6 reshape.33
  69.8 51.2 %all-to-all-done = f32[16,2048,32]{1,2,0:T(8,128)} async-done(((f32[16,2048,32]{1,2,0:T(8,128)}), f32[16,2048,32]{1,2,0:T(8,128)}, u32[]{:S(2)}, u32[]{:S(2)}) %all-to-all-start) | async-done | bytes 4194336 | tf_op jit(solution)/shard_map/all_to_all | solution.py:16
  121.0 9.1 %all-gather.6.cloned.1.call-done = f32[1,1,2048,768]{3,2,1,0:T(8,128)} async-done(((f32[1,1,512,768]{3,2,1,0:T(8,128)}), f32[1,1,2048,768]{3,2,1,0:T(8,128)}) %all-gather.6.cloned.1.call-update) | async-done | bytes 6291472 | tf_op jit(solution)/shard_map/all_gather | solution.py:33
  130.1 13.4 %fusion = f32[512,768]{1,0:T(8,128)S(1)} fusion(f32[2048,512]{0,1:T(8,128)} %bitcast.2, f32[1,1,2048,768]{3,2,1,0:T(8,128)} %all-gather.6.cloned.1.call-done), kind=kOutput, calls=%fused_computation | convolution fusion | flops 9663676416 | bytes 12058624 | tf_op jit(solution)/shard_map/ik,if->kf/dot_general | solution.py:30
  143.5 4.1 %bitcast_divide_fusion = f32[512,768]{1,0:T(8,128)S(1)} fusion(f32[16,32,768]{2,1,0:T(8,128)S(1)} %copy-done.1, f32[512,768]{1,0:T(8,128)S(1)} %fusion, f32[768,768]{1,0:T(8,128)S(1)} %reshape.33), kind=kOutput, calls=%fused_computation.5 | convolution fusion | flops 3624271872 | bytes 7077888 | tf_op jit(solution)/shard_map/dot_general | solution.py:36
  147.6 4.0 %fusion.3 = f32[512,768]{1,0:T(8,128)S(1)} fusion(f32[512,768]{1,0:T(8,128)S(1)} %bitcast_divide_fusion, f32[768,768]{1,0:T(8,128)S(1)} %reshape.33), kind=kOutput, calls=%fused_computation.9 | convolution fusion | flops 3623878656 | bytes 5505024 | tf_op jit(solution)/shard_map/kg,hg->kh/dot_general | solution.py:38
  151.6 14.1 %convolution_bitcast_fusion = f32[2048,768]{0,1:T(8,128)} fusion(f32[512,768]{1,0:T(8,128)S(1)} %fusion.3, f32[2048,512]{0,1:T(8,128)} %bitcast.2), kind=kOutput, calls=%fused_computation.2 | convolution fusion | flops 9663676416 | bytes 12058624 | tf_op jit(solution)/shard_map/dot_general | solution.py:41
  165.7 1.4 copy-done
  167.1 0.5 copy.16
  168.9 61.7 %reduce-scatter.2.cloned.1.call-done = f32[512,768]{0,1:T(8,128)} async-done(((f32[2048,768]{0,1:T(8,128)}), f32[512,768]{0,1:T(8,128)}) %reduce-scatter.2.cloned.1.call-update) | async-done | bytes 1572880 | tf_op jit(solution)/shard_map/reduce_scatter | solution.py:43
  230.6 2.5 fusion.2
  233.0 1.6 copy.17
  235.3 8.5 %psum.14 = f32[32]{0:T(128)S(1)} all-reduce(f32[32]{0:T(128)S(1)} %compare_select_fusion), channel_id=1, replica_groups=mesh['layer'=2,'expert'=16,'matrix'=4] {'matrix'}, use_global_device_ids=true, to_apply=%region_2.0 | all-reduce | flops 32 | bytes 256 | tf_op jit(solution)/shard_map/psum | solution.py:55
  243.8 40.8 %psum.15 = f32[32]{0:T(128)} all-reduce(f32[32]{0:T(128)S(1)} %psum.14), channel_id=1, replica_groups=mesh['layer'=2,'expert'=16,'matrix'=4] {'expert'}, use_global_device_ids=true, to_apply=%region_3.0 | all-reduce | flops 32 | bytes 256 | tf_op jit(solution)/shard_map/psum | solution.py:55
  (11 shorter events, 0.1 us)
Async XLA Ops:
  7.2 55.6 %all-gather.4.cloned.1.call-start = ((), (), s32[]{:S(2)}) async-start(), calls=%async_computation.4 | async-start | bytes 2949120 | tf_op jit(solution)/shard_map/all_gather | solution.py:21
  29.9 1.7 copy-start.2
  30.9 99.2 %all-gather.6.cloned.1.call-start = ((), (), s32[]{:S(2)}) async-start(), calls=%async_computation.6 | async-start | bytes 7864320 | tf_op jit(solution)/shard_map/all_gather | solution.py:33
  56.8 64.2 %all-to-all-start = ((f32[16,2048,32]{1,2,0:T(8,128)}), f32[16,2048,32]{1,2,0:T(8,128)}, u32[]{:S(2)}, u32[]{:S(2)}) async-start(f32[16,2048,32]{1,2,0:T(8,128)} %param.7), calls=%async_computation | async-start | bytes 8388608 | tf_op jit(solution)/shard_map/all_to_all | solution.py:16
  61.4 169.2 %reduce-scatter.2.cloned.1.call-start = ((), (), s32[]{:S(2)}) async-start(), calls=%async_computation.5 | async-start | bytes 7864320 | tf_op jit(solution)/shard_map/reduce_scatter | solution.py:43
  130.1 13.4 %copy-start.1 = (f32[16,32,768]{2,1,0:T(8,128)S(1)}, f32[16,32,768]{2,1,0:T(8,128)}, u32[]{:S(2)}) copy-start(f32[16,32,768]{2,1,0:T(8,128)} %broadcast_add_fusion) | copy-start | bytes 4718596
  165.7 1.4 copy-start
Sparse Core Ops, SparseCore 0:
  31.0 31.6 all-gather.3
  64.3 65.7 all-gather.5
  165.8 64.6 reduce-scatter.1
